TPU v7x, 32 devices: a whole 2x2x4 slice. The times are simulated.
32 devices in a mesh: shard: 2 (over x), rep: 16 (over z, y, core).
Axes of the slice: x: 2, y: 2, z: 4, core: 2. Of those that a mesh axis runs over, the one named last changes fastest.
Arguments:
- frames_in: bfloat16 [16, 1500, 384], P('rep', 'shard'), may hold values from -6 to 6
- params: bfloat16 [2, 1774080], P(None, 'shard'), may hold values from -8 to 8
- moment_one: float32 [2, 1774080], P(None, 'shard'), may hold values from -170.41127 to 170.41127
- moment_two: float32 [2, 1774080], P(None, 'shard'), may hold values from 14.4 to 4800
- cotangent: bfloat16 [16, 1500, 384], P('rep', 'shard'), may hold values from -6 to 6
Outputs:
- encoded: bfloat16 [16, 1500, 384], P('rep', 'shard')
- frames_grad: bfloat16 [16, 1500, 384], P('rep', 'shard')
- param_grad: float32 [2, 1774080], P(None, 'shard')
- new_params: float32 [2, 1774080], P(None, 'shard')
- new_one: float32 [2, 1774080], P(None, 'shard')
- new_two: float32 [2, 1774080], P(None, 'shard')
All inputs are finite; a program needn't handle non-finite values.
Results may differ from a plain program's by a relative error of at most 0.019.
Values may be sent and summed in bfloat16 or wider, within the bound.
A program may use at most 384 MiB of HBM per device.

v0:
```python
from functools import partial

import jax
import jax.numpy as jnp
from jax import lax
from jax.experimental import pallas as pl
from jax.experimental.layout import Layout, with_layout_constraint
from jax.experimental.pallas import tpu as pltpu
from jax.sharding import PartitionSpec as P

D = 384
HEADS = 6
FF = 1536
LAYERS = 2
HD = D // HEADS
LANES = 128
T_QKV, T_O, T_UP, T_DOWN = 3 * D // LANES, D // LANES, FF // LANES, D // LANES
N_QKV, N_O, N_UP, N_DOWN = D * T_QKV, D * T_O, D * T_UP, FF * T_DOWN
N_SMALL = (8 * D + FF) // LANES
N_MAIN = N_O + N_UP + N_DOWN
N_ROWS = N_QKV + N_MAIN + N_SMALL
N_HALF = N_ROWS // 2
UP_BASE, DOWN_BASE = N_O, N_O + N_UP
MESH = pl.DeviceIdType.MESH
CHUNKS = 4
VECS = 16
FB = 384
RC = 256

ln_eps = 1e-05
rate = 0.01
beta_one = 0.9
beta_two = 0.95
adam_eps = 1e-08
decay = 0.1
fix_one = 1.0 - 0.9**3
fix_two = 1.0 - 0.95**3
LOG2E = 1.4426950408889634
SCALE2 = 0.125 * LOG2E
NEG = -1e30

f32 = jnp.float32
bf16 = jnp.bfloat16


def nn(left, right):
    return lax.dot_general(left, right, (((1,), (0,)), ((), ())), preferred_element_type=f32)


def nt(left, right):
    return lax.dot_general(left, right, (((1,), (1,)), ((), ())), preferred_element_type=f32)


def tn(left, right):
    return lax.dot_general(left, right, (((0,), (0,)), ((), ())), preferred_element_type=f32)


def stats(values):
    center = values - jnp.mean(values, axis=-1, keepdims=True)
    r = lax.rsqrt(jnp.mean(center * center, axis=-1, keepdims=True) + ln_eps)
    return center * r, r


def vec(vec_ref, row):
    return vec_ref[row : row + 1, :]


G1, G2, N1, BQ, BV, BO, N2, BD, BUP = range(9)


def each_chunk(rows, body):
    @pl.loop(0, rows // RC)
    def _(i):
        body(pl.ds(pl.multiple_of(i * RC, RC), RC))


def put_row(ref, row, value):
    for j in range(value.shape[1] // LANES):
        ref[pl.ds(row + j, 1), :] = value[:, j * LANES : (j + 1) * LANES]


def put_flat(ref, base, stride, value):
    for j in range(value.shape[1] // LANES):
        ref[pl.ds(base + j, value.shape[0], stride=stride), :] = value[:, j * LANES : (j + 1) * LANES]


def put_up(ref, shift, block, value):
    first = N_HALF - N_QKV - UP_BASE
    whole, edge = first // T_UP, first % T_UP
    for j in range(value.shape[1] // LANES):
        tile = 3 * block + j
        piece = value[:, j * LANES : (j + 1) * LANES]
        at = UP_BASE + tile
        ref[pl.ds(at, whole, stride=T_UP), :] = piece[:whole, :]
        ref[pl.ds(at + T_UP * whole + jnp.where(tile >= edge, shift, 0), 1), :] = piece[whole : whole + 1, :]
        ref[pl.ds(at + T_UP * (whole + 1) + shift, D - whole - 1, stride=T_UP), :] = piece[whole + 1 :, :]


def to_low(src, base, dst, at, count, step=64):
    @pl.loop(0, count // step)
    def _(i):
        dst[pl.ds(pl.multiple_of(at + i * step, 16), step), :] = src[pl.ds(base + i * step, step), :].astype(bf16)


def unpack_weights(flat, outs, stage, which):
    tiles = (T_QKV, T_O, T_UP, T_DOWN)[which]
    base = (0, N_QKV, N_QKV + UP_BASE, N_QKV + DOWN_BASE)[which]
    count = (N_QKV, N_O, N_UP, N_DOWN)[which]

    @pl.loop(0, count // 192)
    def _(i):
        stage[pl.ds(pl.multiple_of(i * 384, 384), 384), :] = flat[
            pl.ds(pl.multiple_of(2 * base + i * 384, 128), 384), :
        ].astype(f32)

    @pl.loop(0, count // tiles // 128)
    def _(i):
        for layer in range(LAYERS):
            for j in range(tiles):
                outs[5 * layer + which][
                    pl.ds(pl.multiple_of(i * 128, 128), 128), j * LANES : (j + 1) * LANES
                ] = stage[pl.ds(i * (256 * tiles) + 2 * j + layer, 128, stride=2 * tiles), :].astype(bf16)


def unpack_small(flat, outs, stage):
    start = N_QKV + N_MAIN
    stage[0 : 2 * N_SMALL, :] = flat[2 * start : 2 * start + 2 * N_SMALL, :].astype(f32)
    for layer in range(LAYERS):
        for i in range(N_SMALL):
            row, j = i // 3, i % 3
            outs[5 * layer + 4][row : row + 1, j * LANES : (j + 1) * LANES] = stage[
                2 * i + layer : 2 * i + layer + 1, :
            ]


def qkv_forward(x_ref, wqkv_ref, vec_ref, q_ref, kv_ref):
    def chunk(rows):
        xhat, _ = stats(x_ref[rows, :].astype(f32))
        a = (xhat * vec(vec_ref, G1) + vec(vec_ref, N1)).astype(bf16)
        qkv = nn(a, wqkv_ref[...])
        q_ref[rows, :] = (qkv[:, :D] + vec(vec_ref, BQ)).astype(bf16)
        kv_ref[0, rows, :] = qkv[:, D : 2 * D].astype(bf16)
        kv_ref[1, rows, :] = (qkv[:, 2 * D :] + vec(vec_ref, BV)).astype(bf16)

    each_chunk(x_ref.shape[0], chunk)


def one_head(values, which):
    lane = lax.broadcasted_iota(jnp.int32, values.shape, 1) - which * HD
    return jnp.where((lane >= 0) & (lane < HD), values, jnp.zeros_like(values))


def pad_mask(scores, rows, pad=None):
    pad = scores.shape[1] if pad is None else pad
    edge = rows // 8 * 8
    keep = lax.broadcasted_iota(jnp.int32, (pad - edge, scores.shape[1]), 0) < rows - edge
    pieces = []
    for base in range(0, scores.shape[0], pad):
        pieces.append(scores[base : base + edge, :])
        pieces.append(jnp.where(keep, scores[base + edge : base + pad, :], NEG))
    return jnp.concatenate(pieces, axis=0)


def attend(q_ref, kv_ref, o_t_ref, lse_ref, values_t, rows):
    pad = q_ref.shape[0]
    values_t[LANES:, :] = jnp.ones((16, 2 * pad), bf16)

    @pl.loop(0, HEADS // 2)
    def _(hp):
        cols = pl.ds(pl.multiple_of(hp * LANES, LANES), LANES)
        values_t[:LANES, :] = jnp.concatenate([kv_ref[0, 1, :, cols], kv_ref[1, 1, :, cols]], axis=0).T

        @pl.loop(0, 2)
        def _(t):
            keys = jnp.concatenate([kv_ref[0, 0, :, cols], kv_ref[1, 0, :, cols]], axis=0)
            scores = pad_mask(nt(keys, one_head(q_ref[:, cols], t)), rows)
            top = jnp.max(scores, axis=0, keepdims=True) * SCALE2
            probs = jnp.exp2(scores * SCALE2 - top).astype(bf16)
            left = jnp.concatenate([values_t[pl.ds(pl.multiple_of(t * HD, HD), HD), :], values_t[LANES:, :]], axis=0)
            mixed = nn(left, probs)
            total = mixed[HD : HD + 1, :]
            head = 2 * hp + t
            o_t_ref[pl.ds(pl.multiple_of(head * HD, HD), HD), :] = (mixed[:HD, :] / total).astype(bf16)
            lse_ref[pl.ds(head, 1), :] = top + jnp.log(total) * LOG2E


def out_forward(x_ref, o_t_ref, wo_ref, vec_ref, h1_ref):
    def chunk(rows):
        h1_ref[rows, :] = x_ref[rows, :].astype(f32) + tn(o_t_ref[:, rows], wo_ref[...]) + vec(vec_ref, BO)

    each_chunk(x_ref.shape[0], chunk)


def second_norm(h1_ref, vec_ref, a2_ref):
    def chunk(rows):
        xhat, _ = stats(h1_ref[rows, :])
        a2_ref[rows, :] = (xhat * vec(vec_ref, G2) + vec(vec_ref, N2)).astype(bf16)

    each_chunk(h1_ref.shape[0], chunk)


def mlp_forward(h1_ref, a2_ref, wup_ref, wdown_ref, vec_ref, x_ref):
    def chunk(rows):
        total = h1_ref[rows, :] + vec(vec_ref, BD)
        for b in range(FF // FB):
            cols = slice(b * FB, (b + 1) * FB)
            u = nn(a2_ref[rows, :], wup_ref[:, cols]) + vec(vec_ref, BUP + b)
            z = (u * (0.5 + 0.5 * lax.erf(u * 0.7071067811865476))).astype(bf16)
            total = total + nn(z, wdown_ref[cols, :])
        x_ref[rows, :] = total.astype(x_ref.dtype)

    each_chunk(h1_ref.shape[0], chunk)


def norm_backward(dy, xhat, r, gain):
    dyg = dy * gain
    inner = jnp.mean(dyg, axis=-1, keepdims=True)
    cross = jnp.mean(dyg * xhat, axis=-1, keepdims=True)
    return r * (dyg - inner - xhat * cross)


def column_sum(values):
    return jnp.sum(values.astype(f32), axis=0, keepdims=True)


def mlp_backward(shift, g_ref, h1_ref, a2_ref, wup_ref, wdown_ref, vec_ref, main_ref, da2_ref, dh1_ref, enc_ref):
    rows_all = g_ref.shape[0]
    small = N_MAIN + shift
    dy2 = g_ref[...].astype(bf16)
    put_row(main_ref, small + 21, column_sum(dy2))
    da2_ref[...] = jnp.zeros_like(da2_ref)
    if enc_ref is not None:
        dh1_ref[...] = h1_ref[...] + vec(vec_ref, BD)

    @pl.loop(0, FF // FB)
    def _(b):
        cols = pl.ds(pl.multiple_of(b * FB, FB), FB)
        u = nn(a2_ref[...], wup_ref[:, cols]) + vec_ref[pl.ds(BUP + b, 1), :]
        cdf = 0.5 + 0.5 * lax.erf(u * 0.7071067811865476)
        z = (u * cdf).astype(bf16)
        slope = cdf + u * jnp.exp2(u * u * (-0.5 * LOG2E)) * 0.3989422804014327
        if enc_ref is not None:
            dh1_ref[...] += nn(z, wdown_ref[cols, :])
        put_flat(main_ref, DOWN_BASE + shift + T_DOWN * FB * b, T_DOWN, tn(z, dy2))
        du = (nt(dy2, wdown_ref[cols, :]) * slope).astype(bf16)
        put_row(main_ref, small + 24 + 3 * b, column_sum(du))
        put_up(main_ref, shift, b, tn(a2_ref[...], du))
        da2_ref[...] += nt(du, wup_ref[:, cols])

    if enc_ref is not None:
        enc_ref[...] = dh1_ref[...].astype(bf16)
    dgain = jnp.zeros((1, D), f32)
    dshift = jnp.zeros((1, D), f32)
    for i in range(rows_all // RC):
        rows = slice(i * RC, (i + 1) * RC)
        xhat, r = stats(h1_ref[rows, :])
        dy = da2_ref[rows, :]
        dgain += column_sum(dy * xhat)
        dshift += column_sum(dy)
        dh1_ref[rows, :] = g_ref[rows, :].astype(f32) + norm_backward(dy, xhat, r, vec(vec_ref, G2))
    put_row(main_ref, small + 3, dgain)
    put_row(main_ref, small + 18, dshift)


def out_backward(shift, dh1_ref, o_t_ref, wo_ref, main_ref, do_ref, delta_ref):
    dy1 = dh1_ref[...].astype(bf16)
    put_row(main_ref, N_MAIN + shift + 15, column_sum(dy1))
    put_flat(main_ref, 0, T_O, nn(o_t_ref[...], dy1))
    do_ref[...] = nt(dy1, wo_ref[...]).astype(bf16)
    do_t = nt(wo_ref[...], dy1).astype(bf16).astype(f32)
    prod = do_t * o_t_ref[...].astype(f32)
    for h in range(HEADS):
        delta_ref[h : h + 1, :] = jnp.sum(prod[h * HD : (h + 1) * HD, :], axis=0, keepdims=True)


def attend_backward(q_ref, kv_ref, lse_ref, do_ref, delta_ref, dq_ref, dkv_ref, dq_t_ref, dk_ref, dv_ref, keys_t,
                    rows, after_pair):
    for hp in range(HEADS // 2):
        cols = slice(hp * LANES, (hp + 1) * LANES)
        dq_t_ref[...] = jnp.zeros_like(dq_t_ref)

        @pl.loop(0, 2)
        def _(half):
            keys_t[...] = kv_ref[half, 0, :, cols].T
            dk_ref[...] = jnp.zeros_like(dk_ref)
            dv_ref[...] = jnp.zeros_like(dv_ref)

            @pl.loop(0, 2)
            def _(t):
                keys, values = kv_ref[half, 0, :, cols], kv_ref[half, 1, :, cols]
                head = pl.ds(2 * hp + t, 1)
                part = pl.ds(pl.multiple_of(t * HD, HD), HD)
                q_one, do_one = one_head(q_ref[:, cols], t), one_head(do_ref[:, cols], t)
                scores = pad_mask(nt(keys, q_one), rows)
                probs = jnp.exp2(scores * SCALE2 - lse_ref[head, :])
                dv_ref[...] += nn(probs.astype(bf16), do_one)
                ds = (probs * (nt(values, do_one) - delta_ref[head, :])).astype(bf16)
                dk_ref[...] += nn(ds, q_one)
                dq_t_ref[part, :] += nn(keys_t[part, :], ds) * 0.125

            dkv_ref[half, 0, :, cols] = (dk_ref[...] * 0.125).astype(bf16)
            dkv_ref[half, 1, :, cols] = dv_ref[...].astype(bf16)

        dq_ref[:, cols] = dq_t_ref[...].T.astype(bf16)
        after_pair(hp)


def qkv_backward(shift, x_ref, dq_ref, dkv_own_ref, dkv_in_ref, dh1_ref, wqkv_ref, vec_ref, gq_ref, tail_ref,
                 a_ref, da_ref, dx_ref):
    def first(rows):
        xhat, _ = stats(x_ref[rows, :].astype(f32))
        a_ref[rows, :] = (xhat * vec(vec_ref, G1) + vec(vec_ref, N1)).astype(bf16)

    each_chunk(x_ref.shape[0], first)
    for b in range(3):
        if b == 0:
            low = dq_ref[...]
        else:
            low = (dkv_own_ref[b - 1].astype(f32) + dkv_in_ref[b - 1].astype(f32)).astype(bf16)
        if b == 0:
            put_row(tail_ref, shift + 9, column_sum(low))
        if b == 2:
            put_row(tail_ref, shift + 12, column_sum(low))
        put_flat(gq_ref, 3 * b, T_QKV, tn(a_ref[...], low))
        part = nt(low, wqkv_ref[:, b * D : (b + 1) * D])
        if b == 0:
            da_ref[...] = part
        else:
            da_ref[...] += part
    dgain = jnp.zeros((1, D), f32)
    dshift = jnp.zeros((1, D), f32)
    for i in range(x_ref.shape[0] // RC):
        rows = slice(i * RC, (i + 1) * RC)
        xhat, r = stats(x_ref[rows, :].astype(f32))
        dy = da_ref[rows, :]
        dgain += column_sum(dy * xhat)
        dshift += column_sum(dy)
        dx_ref[rows, :] = (dh1_ref[rows, :] + norm_backward(dy, xhat, r, vec(vec_ref, G1))).astype(dx_ref.dtype)
    put_row(tail_ref, shift + 0, dgain)
    put_row(tail_ref, shift + 6, dshift)


def meet(partners):
    barrier = pltpu.get_barrier_semaphore()
    for where in partners:
        pl.semaphore_signal(barrier, inc=1, device_id=where, device_id_type=MESH)
    pl.semaphore_wait(barrier, len(partners))


def to(src, dst, send, recv, where):
    return pltpu.make_async_remote_copy(
        src_ref=src, dst_ref=dst, send_sem=send, recv_sem=recv, device_id=where, device_id_type=MESH
    )


def levels_of(ranks):
    bits = ranks.bit_length() - 1
    groups = [(b, min(2, bits - b)) for b in range(2, bits, 2)]
    return [(0, 1), None, (1, 1)] + groups


def peers_of(level):
    low, count = level
    return range(1, 1 << count)


def copies_of(ranks):
    levels = levels_of(ranks)
    down = [2 if k == 0 else 1 if level is None else (1 << level[1]) - 1 for k, level in enumerate(levels)]
    up = [(1 << level[1]) - 1 for level in reversed(levels) if level is not None]
    return down, up


class Reducer:
    def __init__(self, ranks, half_rows, acc, res, landing, send_sems, recv_sems):
        self.acc, self.res, self.landing = acc, res, landing
        self.send_sems, self.recv_sems = send_sems, recv_sems
        self.half_rows = half_rows
        self.n = half_rows // CHUNKS
        self.h = self.n // 2
        self.levels = levels_of(ranks)
        self.back = [level for level in reversed(self.levels) if level is not None]
        self.stages = len(self.levels) + len(self.back)
        down, up = copies_of(ranks)
        self.counts = down + up
        self.state = {}
        self.begun = []

    def place(self):
        return lax.axis_index("shard"), lax.axis_index("rep")

    def index(self, level):
        _, r = self.place()
        return (r >> level[0]) & ((1 << level[1]) - 1)

    def size(self, upto):
        size = self.n
        for level in self.levels[: upto + 1]:
            if level is not None:
                size >>= level[1]
        return size

    def offset(self, upto):
        at = 0
        for k, level in enumerate(self.levels[: upto + 1]):
            if level is not None:
                at = at + self.index(level) * self.size(k)
        return at

    def slot(self, k, m):
        at = 0
        for i in range(k):
            count = self.counts[i]
            at += count * self.size(i)
        return at + m * self.size(k)

    def pair_rows(self, at, size):
        return pl.ds(at // 2 if isinstance(at, int) else lax.div(at, 2), size // 2)

    def acc_at(self, layer, at, size):
        return self.acc.at[self.pair_rows(layer * 2 * self.half_rows + at, size)]

    def describe(self, ci, stage):
        layer, c = ci // CHUNKS, ci % CHUNKS
        base = c * self.n
        s, r = self.place()
        first = sum(self.counts[:stage])
        out = []

        def add(src, dst, where):
            k = first + len(out)
            out.append(to(src, dst, self.send_sems.at[ci, k], self.recv_sems.at[ci, k], where))

        land = lambda k, m: self.landing.at[ci, self.pair_rows(self.slot(k, m), self.size(k))]
        if stage < len(self.levels):
            level = self.levels[stage]
            size = self.size(stage)
            if stage == 0:
                for half in range(2):
                    at = half * self.half_rows + base + (1 - self.index(level)) * size
                    add(self.acc_at(layer, at, size), land(0, half), {"rep": r ^ 1})
            elif level is None:
                at = (1 - s) * self.half_rows + base + self.offset(stage)
                add(self.acc_at(layer, at, size), land(stage, 0), {"shard": 1 - s})
            else:
                for m in peers_of(level):
                    at = s * self.half_rows + base + self.offset(stage - 1) + (self.index(level) ^ m) * size
                    add(self.acc_at(layer, at, size), land(stage, m - 1), {"rep": r ^ (m << level[0])})
        else:
            level = self.back[stage - len(self.levels)]
            k = self.levels.index(level)
            ref = self.res.at[self.pair_rows(layer * self.half_rows + base + self.offset(k), self.size(k))]
            for m in peers_of(level):
                add(ref, ref, {"rep": r ^ (m << level[0])})
        return out

    def begin(self, ci, stage):
        for copy in self.describe(ci, stage):
            copy.start()
        self.begun.append((ci, stage))

    def finish(self, ci, stage):
        layer, c = ci // CHUNKS, ci % CHUNKS
        base = c * self.n
        s, _ = self.place()
        for copy in self.describe(ci, stage):
            copy.wait_recv()
        if stage >= len(self.levels):
            return
        size = self.size(stage)
        acc = self.acc.reshape(2 * self.acc.shape[0], LANES)
        res = self.res.reshape(2 * self.res.shape[0], LANES)
        count = self.landing.shape[1] * 2
        landing = self.landing.reshape(self.landing.shape[0] * count, LANES)
        step = 16
        while size % (2 * step) == 0 and step < 128:
            step *= 2
        last = stage == len(self.levels) - 1
        jobs = []
        if stage == 0:
            for half in range(2):
                jobs.append((half * self.half_rows + base + self.offset(0), [self.slot(0, half)]))
        else:
            jobs.append((s * self.half_rows + base + self.offset(stage),
                         [self.slot(stage, m) for m in range(self.counts[stage])]))
        for at, slots in jobs:
            src = layer * 2 * self.half_rows + at
            out, out_at = acc, src
            if last:
                out, out_at = res, layer * self.half_rows + base + self.offset(stage)

            @pl.loop(0, size // step)
            def _(i):
                def rows(start):
                    return pl.ds(pl.multiple_of(start + i * step, 16), step)

                total = acc[rows(src), :].astype(f32)
                for slot in slots:
                    total = total + landing[rows(ci * count + slot), :].astype(f32)
                out[rows(out_at), :] = total.astype(bf16)

    def advance(self, chunks):
        for ci in chunks:
            stage = self.state.get(ci, -1)
            if stage >= self.stages:
                continue
            if stage >= 0:
                self.finish(ci, stage)
            stage += 1
            self.state[ci] = stage
            if stage < self.stages:
                self.begin(ci, stage)

    def drain(self):
        for ci, stage in self.begun:
            for copy in self.describe(ci, stage):
                copy.wait_send()


def pad_rows(src, dst):
    rows, pad = src.shape[0], dst.shape[0]
    edge = rows // 16 * 16
    dst[:edge, :] = src[:edge, :]
    dst[edge:, :] = jnp.zeros((pad - edge, dst.shape[1]), dst.dtype)
    dst[edge:rows, :] = src[edge:, :]


def step_kernel(ranks, rows, half_rows, frames, cot_in, weights, enc_out, dx_out, out0, out1, x0, cot,
                wqkv0, wo0, wup0, wdown0, vec0, wqkv1, wo1, wup1, wdown1, vec1,
                q0, kv0, o_t0, lse0, h10, x1, q1, kv1, o_t1, lse1, h11, a2, da, dh1,
                do, delta, dq, dkv, dkv_in, dq_t, part_dk, part_dv, keys_t, values_t, enc_in, main, tail, acc, res, landing,
                load, store, swap_sems, rest_sems, hop_sems, kv_sems, send_sems, recv_sems):
    s, r = lax.axis_index("shard"), lax.axis_index("rep")
    shift = half_rows - N_HALF
    across, core, beside = {"shard": 1 - s}, {"rep": r ^ 1}, {"rep": r ^ 2}
    diagonal = {"shard": 1 - s, "rep": r ^ 1}
    stays = s == r % 2
    filling = pltpu.make_async_copy(weights, acc.at[pl.ds(s * N_HALF, N_HALF)], load.at[0])
    filling.start()
    pad_rows(frames, a2)
    pad_rows(cot_in, dq)
    others = [{"rep": r ^ (m << level[0])} for level in levels_of(ranks) if level is not None for m in peers_of(level)]
    meet([diagonal, across] + others)

    def swap(src, dst, k):
        @pl.when(stays)
        def _():
            pltpu.make_async_copy(src, dst, load.at[1 + k]).start()

        @pl.when(jnp.logical_not(stays))
        def _():
            to(src, dst, swap_sems.at[0, k], swap_sems.at[1, k], diagonal).start()

    def swapped(src, dst, k):
        @pl.when(stays)
        def _():
            pltpu.make_async_copy(src, dst, load.at[1 + k]).wait()

        @pl.when(jnp.logical_not(stays))
        def _():
            to(src, dst, swap_sems.at[0, k], swap_sems.at[1, k], diagonal).wait()

    swap(a2, x0, 0)
    filling.wait()
    q = r % 4
    first, second = N_QKV // 4, (N_HALF - N_QKV - N_SMALL) // 4
    parts = []
    for at, quarter in ((0, first), (N_QKV, second)):
        half = quarter // 2
        parts += [(at, quarter, 0, half), (at, quarter, half, quarter - half)]

    def hop(kind, c, half, which, where):
        at, quarter, start, size = parts[c]
        ref = acc.at[pl.ds(half * N_HALF + at + which * quarter + start, size)]
        return to(ref, ref, hop_sems.at[kind, 0, c], hop_sems.at[kind, 1, c], where)

    last = N_QKV + 4 * second
    rest = acc.at[pl.ds(s * N_HALF + last, N_HALF - last)]
    rests = to(rest, rest, rest_sems.at[0], rest_sems.at[1], across)
    rests.start()
    x_hops = [hop(0, c, s, q, across) for c in range(4)]
    y_hops = [hop(1, c, 1 - s, q, beside) for c in range(4)]
    core_hops = [hop(2, c, 1 - s, q, core) for c in range(4)]
    far_hops = [hop(3, c, 1 - s, q ^ 2, core) for c in range(4)]
    for copy in x_hops:
        copy.start()

    def spread(c):
        x_hops[c].wait_recv()
        y_hops[c].start()
        core_hops[c].start()

    def pass_on(c):
        y_hops[c].wait_recv()
        far_hops[c].start()

    def arrived(c):
        core_hops[c].wait_recv()
        far_hops[c].wait_recv()

    outs = [wqkv0, wo0, wup0, wdown0, vec0, wqkv1, wo1, wup1, wdown1, vec1]
    flat = acc.reshape(2 * acc.shape[0], LANES)
    rests.wait_recv()
    unpack_small(flat, outs, main)
    spread(0)
    spread(1)
    pass_on(0)
    pass_on(1)
    arrived(0)
    arrived(1)
    unpack_weights(flat, outs, main, 0)
    spread(2)

    exchanges = []

    def exchange(src, dst):
        k = len(exchanges)
        copy = to(src, dst, kv_sems.at[0, k], kv_sems.at[1, k], core)
        copy.start()
        exchanges.append(copy)
        return copy

    swapped(a2, x0, 0)
    qkv_forward(x0, wqkv0, vec0, q0, kv0.at[0])
    first_kv = exchange(kv0.at[0], kv0.at[1])
    spread(3)
    swap(dq, cot, 1)
    first_kv.wait_recv()
    attend(q0, kv0, o_t0, lse0, values_t, rows)
    pass_on(2)
    pass_on(3)
    arrived(2)
    arrived(3)
    for copy in x_hops + y_hops + core_hops + far_hops + [rests]:
        copy.wait_send()
    for which in (1, 2, 3):
        unpack_weights(flat, outs, main, which)
    out_forward(x0, o_t0, wo0, vec0, h10)
    second_norm(h10, vec0, a2)
    mlp_forward(h10, a2, wup0, wdown0, vec0, x1)
    qkv_forward(x1, wqkv1, vec1, q1, kv1.at[0])
    exchange(kv1.at[0], kv1.at[1]).wait_recv()
    attend(q1, kv1, o_t1, lse1, values_t, rows)
    out_forward(x1, o_t1, wo1, vec1, h11)
    second_norm(h11, vec1, a2)

    enc = wdown1.at[pl.ds(0, x0.shape[0])]
    reducer = Reducer(ranks, half_rows, acc, res, landing, send_sems, recv_sems)
    early = [[layer * CHUNKS + c for c in range(CHUNKS // 2, CHUNKS)] for layer in range(LAYERS)]
    late = [[layer * CHUNKS + c for c in range(CHUNKS // 2)] for layer in range(LAYERS)]
    moved = (N_MAIN + shift) // 16 * 16

    def main_start():
        edge = N_HALF - N_QKV
        main[edge : edge + shift, :] = jnp.zeros((shift, LANES), f32)
        last = N_MAIN + shift
        main[last:, :] = jnp.zeros((main.shape[0] - last, LANES), f32)

    def main_end(layer):
        base = layer * 2 * half_rows
        to_low(main, 0, flat, base + N_QKV, main.shape[0])
        to_low(main, half_rows - N_QKV, flat, base + N_QKV + moved, 32, 32)
        tail[...] = main[moved : moved + 32, :]

    def late_end(layer):
        base = layer * 2 * half_rows
        to_low(main, 0, flat, base, N_QKV)
        to_low(tail, 0, flat, base + half_rows, 32, 32)

    tail_shift = N_MAIN + shift - moved
    main_start()
    swapped(dq, cot, 1)
    mlp_backward(shift, cot, h11, a2, wup1, wdown1, vec1, main, da, dh1, enc)
    swap(enc, enc_in, 2)
    out_backward(shift, dh1, o_t1, wo1, main, do, delta)
    main_end(1)
    reducer.advance(early[1])
    attend_backward(q1, kv1, lse1, do, delta, dq, dkv, dq_t, part_dk, part_dv, keys_t, rows,
                    lambda hp: reducer.advance(early[1]))
    exchange(dkv.at[1], dkv_in).wait_recv()
    qkv_backward(tail_shift, x1, dq, dkv.at[0], dkv_in, dh1, wqkv1, vec1, main, tail, a2, da, h11)
    late_end(1)
    reducer.advance(early[1])
    reducer.advance(late[1])
    main_start()
    second_norm(h10, vec0, a2)
    reducer.advance(late[1])
    exchanges[-1].wait_send()
    mlp_backward(shift, h11, h10, a2, wup0, wdown0, vec0, main, da, dh1, None)
    reducer.advance(early[1])
    out_backward(shift, dh1, o_t0, wo0, main, do, delta)
    main_end(0)
    reducer.advance(late[1])
    reducer.advance(early[0])
    attend_backward(q0, kv0, lse0, do, delta, dq, dkv, dq_t, part_dk, part_dv, keys_t, rows,
                    lambda hp: reducer.advance(early[1] + late[1] + early[0]))
    exchange(dkv.at[1], kv1.at[1]).wait_recv()
    qkv_backward(tail_shift, x0, dq, dkv.at[0], kv1.at[1], dh1, wqkv0, vec0, main, tail, a2, da, do)
    swap(do, cot, 3)
    late_end(0)
    for tick in range(reducer.stages + 2):
        reducer.advance(early[1] + late[1] + early[0])
        for k, ci in enumerate(late[0]):
            if tick >= k:
                reducer.advance([ci])
    reducer.drain()
    for k, copy in enumerate(exchanges):
        if k != 2:
            copy.wait_send()

    @pl.when(s == 1)
    def _():
        out = res.reshape(2 * res.shape[0], LANES)
        for layer in range(LAYERS):
            one = pl.ds(layer * half_rows, 32)
            two = pl.ds(layer * half_rows + N_QKV + moved - half_rows, 32)
            keep = out[one, :]
            out[one, :] = out[two, :]
            out[two, :] = keep

    outs = [
        pltpu.make_async_copy(res.at[pl.ds(k * half_rows // 2, half_rows // 2)], out, store.at[k])
        for k, out in enumerate((out0, out1))
    ]
    for copy in outs:
        copy.start()
    swapped(enc, enc_in, 2)
    enc_out[...] = enc_in[:rows, :]
    swapped(do, cot, 3)
    dx_out[...] = cot[:rows, :]
    for copy in outs:
        copy.wait()


def adam_kernel(g0_ref, g1_ref, w_ref, one_ref, two_ref, g_out, p_out, one_out, two_out):
    block = 2 * g0_ref.shape[0]
    flat = lambda ref: ref.reshape(LAYERS * block, LANES)
    low = lambda ref: ref.reshape(block, LANES)
    for layer, g_ref in enumerate((g0_ref, g1_ref)):
        flat(g_out)[pl.ds(layer, block, stride=LAYERS), :] = low(g_ref)[...].astype(f32)

    @pl.loop(0, LAYERS * block // 128)
    def _(i):
        rows = pl.ds(pl.multiple_of(i * 128, 128), 128)
        grad = flat(g_out)[rows, :]
        weight = flat(w_ref)[rows, :].astype(f32)
        one = beta_one * flat(one_ref)[rows, :] + (1.0 - beta_one) * grad
        two = beta_two * flat(two_ref)[rows, :] + (1.0 - beta_two) * grad * grad
        step = (one * (1.0 / fix_one)) / (jnp.sqrt(two * (1.0 / fix_two)) + adam_eps) + decay * weight
        flat(p_out)[rows, :] = weight - rate * step
        flat(one_out)[rows, :] = one
        flat(two_out)[rows, :] = two


def to_rows(array):
    view = array.reshape(LAYERS, -1, LANES)
    return with_layout_constraint(view, Layout(major_to_minor=(1, 0, 2))).transpose(1, 0, 2)


def from_rows(array):
    view = with_layout_constraint(array.transpose(1, 0, 2), Layout(major_to_minor=(1, 0, 2)))
    return view.reshape(LAYERS, -1)


def body(ranks, frames_in, params, moment_one, moment_two, cotangent):
    rows = frames_in.shape[1]
    pad = -(-rows // RC) * RC

    def vm(shape, dtype):
        return pltpu.VMEM(shape, dtype)

    def sd(shape, dtype):
        return jax.ShapeDtypeStruct(shape, dtype)

    unit = 16 * ranks * CHUNKS
    half_rows = -(-N_HALF // unit) * unit
    tail_rows = -(-(half_rows - N_HALF + N_SMALL + 32) // 64) * 64
    w_rows = to_rows(params)
    row_b = vm((pad, D), bf16)
    kv_b = vm((2, pad, D), bf16)
    kv_both = vm((2, 2, pad, D), bf16)
    row_f = vm((pad, D), f32)
    lse_f = vm((8, pad), f32)
    o_t_b = vm((D, pad), bf16)
    layer_w = [vm((D, 3 * D), bf16), vm((D, D), bf16), vm((D, FF), bf16), vm((FF, D), bf16), vm((VECS, D), f32)]
    down, up = copies_of(ranks)
    total = LAYERS * CHUNKS
    chunk_sems = pltpu.SemaphoreType.DMA((total, sum(down) + sum(up)))
    anywhere = pl.BlockSpec(memory_space=pl.ANY)
    inside = pl.BlockSpec(memory_space=pltpu.VMEM)
    enc, dx, g0, g1 = pl.pallas_call(
        partial(step_kernel, ranks, rows, half_rows),
        out_shape=[sd((rows, D), bf16)] * 2 + [sd((half_rows // 2, 2, LANES), bf16)] * 2,
        in_specs=[inside, inside, anywhere],
        out_specs=[inside] * 2 + [anywhere] * 2,
        scratch_shapes=[row_b, row_b] + layer_w * 2
        + [row_b, kv_both, o_t_b, lse_f, row_f, row_f, row_b, kv_both, o_t_b, lse_f, row_f, row_b]
        + [row_f, row_f, row_b, lse_f, row_b, kv_both, kv_b]
        + [vm((LANES, pad), f32), vm((pad, LANES), f32), vm((pad, LANES), f32), vm((LANES, pad), bf16), vm((LANES + 16, 2 * pad), bf16), row_b]
        + [vm((N_MAIN + tail_rows, LANES), f32), vm((32, LANES), f32), vm((2 * half_rows, 2, LANES), bf16)]
        + [vm((half_rows, 2, LANES), bf16), vm((total, half_rows // CHUNKS, 2, LANES), bf16)]
        + [pltpu.SemaphoreType.DMA((5,)), pltpu.SemaphoreType.DMA((2,)), pltpu.SemaphoreType.DMA((2, 4))]
        + [pltpu.SemaphoreType.DMA((2,)), pltpu.SemaphoreType.DMA((4, 2, 4)), pltpu.SemaphoreType.DMA((2, 4))]
        + [chunk_sems, chunk_sems],
        compiler_params=pltpu.CompilerParams(vmem_limit_bytes=67043328, collective_id=0, has_side_effects=True),
        name="step",
    )(frames_in[0], cotangent[0], w_rows)
    encoded, frames_grad = enc[None], dx[None]
    block = 640
    low = pl.BlockSpec((block // 2, 2, LANES), lambda i: (i, 0, 0))
    spec = pl.BlockSpec((block, 2, LANES), lambda i: (i, 0, 0))
    row_shape = sd((N_HALF, 2, LANES), f32)
    grad, new_params, new_one, new_two = pl.pallas_call(
        adam_kernel, grid=(pl.cdiv(N_HALF, block),), in_specs=[low, low, spec, spec, spec], out_specs=[spec] * 4,
        out_shape=[row_shape] * 4,
        compiler_params=pltpu.CompilerParams(vmem_limit_bytes=62 << 20), name="adam",
    )(g0, g1, w_rows, to_rows(moment_one), to_rows(moment_two))
    return (encoded, frames_grad, from_rows(grad), from_rows(new_params), from_rows(new_one), from_rows(new_two))


def solution(mesh):
    in_specs = (
        P("rep", "shard", None),
        P(None, "shard"),
        P(None, "shard"),
        P(None, "shard"),
        P("rep", "shard", None),
    )
    out_specs = (
        P("rep", "shard", None),
        P("rep", "shard", None),
        P(None, "shard"),
        P(None, "shard"),
        P(None, "shard"),
        P(None, "shard"),
    )
    return jax.shard_map(
        partial(body, mesh.shape["rep"]), mesh=mesh, in_specs=in_specs, out_specs=out_specs, check_vma=False
    )
```

profile of v0, /device:TPU:1, one launch (start us, length us, event | category | flops | bytes accessed | tf_op | source)
XLA Modules:
  0.0 257.2 jit_solution(8965130715108058226)
XLA Ops:
  0.6 230.1 %step.1 = (bf16[750,384]{1,0:T(8,128)(2,1)}, bf16[750,384]{1,0:T(8,128)(2,1)}, bf16[3584,2,128]{2,1,0:T(2,128)(2,1)}, bf16[3584,2,128]{2,1,0:T(2,128)(2,1)}) custom-call(bf16[750,384]{1,0:T(8,128)(2,1)} %bitcast.29, bf16[750,384]{1,0:T(8,128)(2,1)} %bitcast.30, bf16[6930,2,128]{2,1,0:T(2,128)(2,1)} %bitcast.25), custom_call_target="tpu_custom_call" | custom-call | tf_op jit(solution)/shard_map/step/pallas_call | solution.py:791
  230.8 0.0 copy-start.1
  230.8 0.0 copy-start
  230.8 24.8 %adam.1 = (f32[6930,2,128]{2,1,0:T(2,128)}, f32[6930,2,128]{2,1,0:T(2,128)}, f32[6930,2,128]{2,1,0:T(2,128)}, f32[6930,2,128]{2,1,0:T(2,128)}) custom-call(bf16[3584,2,128]{2,1,0:T(2,128)(2,1)} %get-tuple-element.16.g0_ref, bf16[3584,2,128]{2,1,0:T(2,128)(2,1)} %get-tuple-element.17.g1_ref, bf16[6930,2,128]{2,1,0:T(2,128)(2,1)} %bitcast.26, ...), custom_call_target="tpu_custom_call" | custom-call | tf_op jit(solution)/shard_map/adam/pallas_call | solution.py:813
  255.6 0.0 copy-done.1
  255.6 0.8 copy.13
  256.4 0.0 copy-done
  256.4 0.8 copy.14
Async XLA Ops:
  230.8 24.8 %copy-start.1 = (bf16[750,384]{1,0:T(8,128)(2,1)S(1)}, bf16[750,384]{1,0:T(8,128)(2,1)}, u32[]{:S(2)}) copy-start(bf16[750,384]{1,0:T(8,128)(2,1)} %get-tuple-element.14) | copy-start | bytes 1728004
  230.8 25.6 %copy-start = (bf16[750,384]{1,0:T(8,128)(2,1)S(1)}, bf16[750,384]{1,0:T(8,128)(2,1)}, u32[]{:S(2)}) copy-start(bf16[750,384]{1,0:T(8,128)(2,1)} %get-tuple-element.15) | copy-start | bytes 1728004
where the time goes:
time: 258 us; the launch traced here: 257 us
  Pallas kernels  255 us (99%)
    pallas_call x1, Pallas kernels, body(): pl.pallas_call(partial(step_kernel, ranks, rows, half_rows), out_shape=[s...  230 us
    pallas_call x1, Pallas kernels, body(): pl.pallas_call(adam_kernel, grid=(pl.cdiv(N_HALF, block),), in_specs=[low...  24.8 us

commit v1 on v0

--- a/solution.py
+++ b/solution.py
@@ -161,7 +161,7 @@
     return jnp.concatenate(pieces, axis=0)
 
 
-def attend(q_ref, kv_ref, o_t_ref, lse_ref, values_t, rows):
+def attend(q_ref, kv_ref, o_t_ref, lse_ref, values_t, rows, after_pair=None):
     pad = q_ref.shape[0]
     values_t[LANES:, :] = jnp.ones((16, 2 * pad), bf16)
 
@@ -183,6 +183,12 @@
             o_t_ref[pl.ds(pl.multiple_of(head * HD, HD), HD), :] = (mixed[:HD, :] / total).astype(bf16)
             lse_ref[pl.ds(head, 1), :] = top + jnp.log(total) * LOG2E
 
+        for k in range(HEADS // 2 if after_pair else 0):
+
+            @pl.when(hp == k)
+            def _():
+                after_pair(k)
+
 
 def out_forward(x_ref, o_t_ref, wo_ref, vec_ref, h1_ref):
     def chunk(rows):
@@ -200,16 +206,14 @@
 
 
 def mlp_forward(h1_ref, a2_ref, wup_ref, wdown_ref, vec_ref, x_ref):
-    def chunk(rows):
-        total = h1_ref[rows, :] + vec(vec_ref, BD)
-        for b in range(FF // FB):
-            cols = slice(b * FB, (b + 1) * FB)
-            u = nn(a2_ref[rows, :], wup_ref[:, cols]) + vec(vec_ref, BUP + b)
-            z = (u * (0.5 + 0.5 * lax.erf(u * 0.7071067811865476))).astype(bf16)
-            total = total + nn(z, wdown_ref[cols, :])
-        x_ref[rows, :] = total.astype(x_ref.dtype)
-
-    each_chunk(h1_ref.shape[0], chunk)
+    x_ref[...] = h1_ref[...] + vec(vec_ref, BD)
+
+    @pl.loop(0, FF // FB)
+    def _(b):
+        cols = pl.ds(pl.multiple_of(b * FB, FB), FB)
+        u = nn(a2_ref[...], wup_ref[:, cols]) + vec_ref[pl.ds(BUP + b, 1), :]
+        z = (u * (0.5 + 0.5 * lax.erf(u * 0.7071067811865476))).astype(bf16)
+        x_ref[...] += nn(z, wdown_ref[cols, :])
 
 
 def norm_backward(dy, xhat, r, gain):
@@ -273,60 +277,63 @@
         delta_ref[h : h + 1, :] = jnp.sum(prod[h * HD : (h + 1) * HD, :], axis=0, keepdims=True)
 
 
-def attend_backward(q_ref, kv_ref, lse_ref, do_ref, delta_ref, dq_ref, dkv_ref, dq_t_ref, dk_ref, dv_ref, keys_t,
-                    rows, after_pair):
-    for hp in range(HEADS // 2):
-        cols = slice(hp * LANES, (hp + 1) * LANES)
-        dq_t_ref[...] = jnp.zeros_like(dq_t_ref)
-
-        @pl.loop(0, 2)
-        def _(half):
-            keys_t[...] = kv_ref[half, 0, :, cols].T
-            dk_ref[...] = jnp.zeros_like(dk_ref)
-            dv_ref[...] = jnp.zeros_like(dv_ref)
-
-            @pl.loop(0, 2)
-            def _(t):
-                keys, values = kv_ref[half, 0, :, cols], kv_ref[half, 1, :, cols]
+def attend_backward(q_ref, kv_ref, lse_ref, do_ref, delta_ref, dqkv_ref, dkv_oth_ref, dq_t_ref, rows, after_pair):
+    @pl.loop(0, HEADS // 2)
+    def _(hp):
+        cols = pl.ds(pl.multiple_of(hp * LANES, LANES), LANES)
+        for half in range(2):
+            keys, values = kv_ref[half, 0, :, cols], kv_ref[half, 1, :, cols]
+            keys_t = keys.T
+            dk = dv = 0.0
+            for t in range(2):
                 head = pl.ds(2 * hp + t, 1)
-                part = pl.ds(pl.multiple_of(t * HD, HD), HD)
+                part = slice(t * HD, (t + 1) * HD)
                 q_one, do_one = one_head(q_ref[:, cols], t), one_head(do_ref[:, cols], t)
                 scores = pad_mask(nt(keys, q_one), rows)
                 probs = jnp.exp2(scores * SCALE2 - lse_ref[head, :])
-                dv_ref[...] += nn(probs.astype(bf16), do_one)
+                dv += nn(probs.astype(bf16), do_one)
                 ds = (probs * (nt(values, do_one) - delta_ref[head, :])).astype(bf16)
-                dk_ref[...] += nn(ds, q_one)
-                dq_t_ref[part, :] += nn(keys_t[part, :], ds) * 0.125
-
-            dkv_ref[half, 0, :, cols] = (dk_ref[...] * 0.125).astype(bf16)
-            dkv_ref[half, 1, :, cols] = dv_ref[...].astype(bf16)
-
-        dq_ref[:, cols] = dq_t_ref[...].T.astype(bf16)
-        after_pair(hp)
-
-
-def qkv_backward(shift, x_ref, dq_ref, dkv_own_ref, dkv_in_ref, dh1_ref, wqkv_ref, vec_ref, gq_ref, tail_ref,
-                 a_ref, da_ref, dx_ref):
+                dk += nn(ds, q_one)
+                dq_part = nn(keys_t[part, :], ds) * 0.125
+                if half == 0:
+                    dq_t_ref[part, :] = dq_part
+                else:
+                    dq_t_ref[part, :] += dq_part
+            dst = (dqkv_ref.at[pl.ds(1, 2)], dkv_oth_ref)[half]
+            dst[0, :, cols] = (dk * 0.125).astype(bf16)
+            dst[1, :, cols] = dv.astype(bf16)
+        dqkv_ref[0, :, cols] = dq_t_ref[...].T.astype(bf16)
+        for k in range(HEADS // 2):
+
+            @pl.when(hp == k)
+            def _():
+                after_pair(k)
+
+
+def qkv_backward(shift, x_ref, dqkv_ref, dkv_in_ref, dh1_ref, wqkv_ref, vec_ref, gq_ref, tail_ref,
+                 a_ref, da_ref, dx_ref, after_blocks):
     def first(rows):
         xhat, _ = stats(x_ref[rows, :].astype(f32))
         a_ref[rows, :] = (xhat * vec(vec_ref, G1) + vec(vec_ref, N1)).astype(bf16)
+        for b in range(2):
+            total = dqkv_ref[b + 1, rows, :].astype(f32) + dkv_in_ref[b, rows, :].astype(f32)
+            dqkv_ref[b + 1, rows, :] = total.astype(bf16)
 
     each_chunk(x_ref.shape[0], first)
-    for b in range(3):
-        if b == 0:
-            low = dq_ref[...]
-        else:
-            low = (dkv_own_ref[b - 1].astype(f32) + dkv_in_ref[b - 1].astype(f32)).astype(bf16)
-        if b == 0:
-            put_row(tail_ref, shift + 9, column_sum(low))
-        if b == 2:
-            put_row(tail_ref, shift + 12, column_sum(low))
+    da_ref[...] = jnp.zeros_like(da_ref)
+
+    @pl.loop(0, 3)
+    def _(b):
+        low = dqkv_ref[b]
+
+        @pl.when(b != 1)
+        def _():
+            put_row(tail_ref, shift + 9 + jnp.where(b == 2, 3, 0), column_sum(low))
+
         put_flat(gq_ref, 3 * b, T_QKV, tn(a_ref[...], low))
-        part = nt(low, wqkv_ref[:, b * D : (b + 1) * D])
-        if b == 0:
-            da_ref[...] = part
-        else:
-            da_ref[...] += part
+        da_ref[...] += nt(low, wqkv_ref[:, pl.ds(pl.multiple_of(b * D, D), D)])
+
+    after_blocks()
     dgain = jnp.zeros((1, D), f32)
     dshift = jnp.zeros((1, D), f32)
     for i in range(x_ref.shape[0] // RC):
@@ -340,11 +347,9 @@
     put_row(tail_ref, shift + 6, dshift)
 
 
-def meet(partners):
-    barrier = pltpu.get_barrier_semaphore()
+def greet(partners):
     for where in partners:
-        pl.semaphore_signal(barrier, inc=1, device_id=where, device_id_type=MESH)
-    pl.semaphore_wait(barrier, len(partners))
+        pl.semaphore_signal(pltpu.get_barrier_semaphore(), inc=1, device_id=where, device_id_type=MESH)
 
 
 def to(src, dst, send, recv, where):
@@ -353,10 +358,10 @@
     )
 
 
-def levels_of(ranks):
+def levels_of(ranks, late_x=False):
     bits = ranks.bit_length() - 1
     groups = [(b, min(2, bits - b)) for b in range(2, bits, 2)]
-    return [(0, 1), None, (1, 1)] + groups
+    return [(0, 1), (1, 1), None] + groups if late_x else [(0, 1), None, (1, 1)] + groups
 
 
 def peers_of(level):
@@ -364,9 +369,11 @@
     return range(1, 1 << count)
 
 
-def copies_of(ranks):
-    levels = levels_of(ranks)
-    down = [2 if k == 0 else 1 if level is None else (1 << level[1]) - 1 for k, level in enumerate(levels)]
+def copies_of(levels):
+    crossing = levels.index(None)
+    down = []
+    for k, level in enumerate(levels):
+        down.append(1 if level is None else ((1 << level[1]) - 1) * (2 if k < crossing else 1))
     up = [(1 << level[1]) - 1 for level in reversed(levels) if level is not None]
     return down, up
 
@@ -377,14 +384,15 @@
         self.send_sems, self.recv_sems = send_sems, recv_sems
         self.half_rows = half_rows
         self.n = half_rows // CHUNKS
-        self.h = self.n // 2
-        self.levels = levels_of(ranks)
-        self.back = [level for level in reversed(self.levels) if level is not None]
-        self.stages = len(self.levels) + len(self.back)
-        down, up = copies_of(ranks)
-        self.counts = down + up
+        self.orders = [levels_of(ranks), levels_of(ranks, True)]
+        self.stages = 2 * len(self.orders[0]) - 1
         self.state = {}
         self.begun = []
+
+    def plan(self, ci):
+        levels = self.orders[ci % 2]
+        down, up = copies_of(levels)
+        return levels, down + up
 
     def place(self):
         return lax.axis_index("shard"), lax.axis_index("rep")
@@ -393,63 +401,56 @@
         _, r = self.place()
         return (r >> level[0]) & ((1 << level[1]) - 1)
 
-    def size(self, upto):
+    def size(self, levels, upto):
         size = self.n
-        for level in self.levels[: upto + 1]:
+        for level in levels[: upto + 1]:
             if level is not None:
                 size >>= level[1]
         return size
 
-    def offset(self, upto):
+    def offset(self, levels, upto):
         at = 0
-        for k, level in enumerate(self.levels[: upto + 1]):
+        for k, level in enumerate(levels[: upto + 1]):
             if level is not None:
-                at = at + self.index(level) * self.size(k)
+                at = at + self.index(level) * self.size(levels, k)
         return at
 
-    def slot(self, k, m):
-        at = 0
-        for i in range(k):
-            count = self.counts[i]
-            at += count * self.size(i)
-        return at + m * self.size(k)
+    def slot(self, ci, k, m):
+        levels, counts = self.plan(ci)
+        return sum(counts[i] * self.size(levels, i) for i in range(k)) + m * self.size(levels, k)
 
     def pair_rows(self, at, size):
         return pl.ds(at // 2 if isinstance(at, int) else lax.div(at, 2), size // 2)
 
-    def acc_at(self, layer, at, size):
-        return self.acc.at[self.pair_rows(layer * 2 * self.half_rows + at, size)]
-
     def describe(self, ci, stage):
-        layer, c = ci // CHUNKS, ci % CHUNKS
-        base = c * self.n
+        layer, base = ci // CHUNKS, ci % CHUNKS * self.n
+        levels, counts = self.plan(ci)
         s, r = self.place()
-        first = sum(self.counts[:stage])
+        first = sum(counts[:stage])
         out = []
 
         def add(src, dst, where):
             k = first + len(out)
             out.append(to(src, dst, self.send_sems.at[ci, k], self.recv_sems.at[ci, k], where))
 
-        land = lambda k, m: self.landing.at[ci, self.pair_rows(self.slot(k, m), self.size(k))]
-        if stage < len(self.levels):
-            level = self.levels[stage]
-            size = self.size(stage)
-            if stage == 0:
-                for half in range(2):
-                    at = half * self.half_rows + base + (1 - self.index(level)) * size
-                    add(self.acc_at(layer, at, size), land(0, half), {"rep": r ^ 1})
-            elif level is None:
-                at = (1 - s) * self.half_rows + base + self.offset(stage)
-                add(self.acc_at(layer, at, size), land(stage, 0), {"shard": 1 - s})
+        def send(half, at, size, where):
+            rows = self.pair_rows((layer * 2 + half) * self.half_rows + base + at, size)
+            add(self.acc.at[rows], self.landing.at[ci, self.pair_rows(self.slot(ci, stage, len(out)), size)], where)
+
+        if stage < len(levels):
+            level, size = levels[stage], self.size(levels, stage)
+            if level is None:
+                send(1 - s, self.offset(levels, stage), size, {"shard": 1 - s})
             else:
-                for m in peers_of(level):
-                    at = s * self.half_rows + base + self.offset(stage - 1) + (self.index(level) ^ m) * size
-                    add(self.acc_at(layer, at, size), land(stage, m - 1), {"rep": r ^ (m << level[0])})
+                for half in range(2) if stage < levels.index(None) else (s,):
+                    for m in peers_of(level):
+                        at = self.offset(levels, stage - 1) + (self.index(level) ^ m) * size
+                        send(half, at, size, {"rep": r ^ (m << level[0])})
         else:
-            level = self.back[stage - len(self.levels)]
-            k = self.levels.index(level)
-            ref = self.res.at[self.pair_rows(layer * self.half_rows + base + self.offset(k), self.size(k))]
+            level = [one for one in reversed(levels) if one is not None][stage - len(levels)]
+            k = levels.index(level)
+            at = layer * self.half_rows + base + self.offset(levels, k)
+            ref = self.res.at[self.pair_rows(at, self.size(levels, k))]
             for m in peers_of(level):
                 add(ref, ref, {"rep": r ^ (m << level[0])})
         return out
@@ -460,14 +461,14 @@
         self.begun.append((ci, stage))
 
     def finish(self, ci, stage):
-        layer, c = ci // CHUNKS, ci % CHUNKS
-        base = c * self.n
+        layer, base = ci // CHUNKS, ci % CHUNKS * self.n
+        levels, counts = self.plan(ci)
         s, _ = self.place()
         for copy in self.describe(ci, stage):
             copy.wait_recv()
-        if stage >= len(self.levels):
+        if stage >= len(levels):
             return
-        size = self.size(stage)
+        size = self.size(levels, stage)
         acc = self.acc.reshape(2 * self.acc.shape[0], LANES)
         res = self.res.reshape(2 * self.res.shape[0], LANES)
         count = self.landing.shape[1] * 2
@@ -475,19 +476,14 @@
         step = 16
         while size % (2 * step) == 0 and step < 128:
             step *= 2
-        last = stage == len(self.levels) - 1
-        jobs = []
-        if stage == 0:
-            for half in range(2):
-                jobs.append((half * self.half_rows + base + self.offset(0), [self.slot(0, half)]))
-        else:
-            jobs.append((s * self.half_rows + base + self.offset(stage),
-                         [self.slot(stage, m) for m in range(self.counts[stage])]))
-        for at, slots in jobs:
-            src = layer * 2 * self.half_rows + at
+        halves = (0, 1) if stage < levels.index(None) else (s,)
+        each = counts[stage] // len(halves)
+        for k, half in enumerate(halves):
+            slots = [self.slot(ci, stage, k * each + m) for m in range(each)]
+            src = (layer * 2 + half) * self.half_rows + base + self.offset(levels, stage)
             out, out_at = acc, src
-            if last:
-                out, out_at = res, layer * self.half_rows + base + self.offset(stage)
+            if stage == len(levels) - 1:
+                out, out_at = res, layer * self.half_rows + base + self.offset(levels, stage)
 
             @pl.loop(0, size // step)
             def _(i):
@@ -528,8 +524,8 @@
 def step_kernel(ranks, rows, half_rows, frames, cot_in, weights, enc_out, dx_out, out0, out1, x0, cot,
                 wqkv0, wo0, wup0, wdown0, vec0, wqkv1, wo1, wup1, wdown1, vec1,
                 q0, kv0, o_t0, lse0, h10, x1, q1, kv1, o_t1, lse1, h11, a2, da, dh1,
-                do, delta, dq, dkv, dkv_in, dq_t, part_dk, part_dv, keys_t, values_t, enc_in, main, tail, acc, res, landing,
-                load, store, swap_sems, rest_sems, hop_sems, kv_sems, send_sems, recv_sems):
+                do, delta, dq, dqkv, dkv_oth, dkv_in, dq_t, values_t, enc_in, main, tail, acc, res, landing,
+                load, store, swap_sems, relay_sems, rest_sems, hop_sems, kv_sems, send_sems, recv_sems):
     s, r = lax.axis_index("shard"), lax.axis_index("rep")
     shift = half_rows - N_HALF
     across, core, beside = {"shard": 1 - s}, {"rep": r ^ 1}, {"rep": r ^ 2}
@@ -537,10 +533,20 @@
     stays = s == r % 2
     filling = pltpu.make_async_copy(weights, acc.at[pl.ds(s * N_HALF, N_HALF)], load.at[0])
     filling.start()
+    partners = [{"rep": r ^ (m << level[0])} for level in levels_of(ranks) if level is not None for m in peers_of(level)]
+    partners += [diagonal, across]
+    greet(partners)
+    outs = [wqkv0, wo0, wup0, wdown0, vec0, wqkv1, wo1, wup1, wdown1, vec1]
+    flat = acc.reshape(2 * acc.shape[0], LANES)
     pad_rows(frames, a2)
     pad_rows(cot_in, dq)
-    others = [{"rep": r ^ (m << level[0])} for level in levels_of(ranks) if level is not None for m in peers_of(level)]
-    meet([diagonal, across] + others)
+    filling.wait()
+
+    @pl.when(s == 0)
+    def _():
+        unpack_weights(flat, outs, main, 0)
+
+    pl.semaphore_wait(pltpu.get_barrier_semaphore(), len(partners))
 
     def swap(src, dst, k):
         @pl.when(stays)
@@ -560,56 +566,104 @@
         def _():
             to(src, dst, swap_sems.at[0, k], swap_sems.at[1, k], diagonal).wait()
 
-    swap(a2, x0, 0)
-    filling.wait()
     q = r % 4
-    first, second = N_QKV // 4, (N_HALF - N_QKV - N_SMALL) // 4
-    parts = []
-    for at, quarter in ((0, first), (N_QKV, second)):
-        half = quarter // 2
-        parts += [(at, quarter, 0, half), (at, quarter, half, quarter - half)]
-
-    def hop(kind, c, half, which, where):
-        at, quarter, start, size = parts[c]
-        ref = acc.at[pl.ds(half * N_HALF + at + which * quarter + start, size)]
-        return to(ref, ref, hop_sems.at[kind, 0, c], hop_sems.at[kind, 1, c], where)
-
+    second = (N_HALF - N_QKV - N_SMALL) // 4
     last = N_QKV + 4 * second
+    part = D // 4
+
+    def flow(kind, c, which):
+        return (hop_sems.at[kind, 0, c], hop_sems.at[kind, 1, c], (across, beside, core, core)[kind])
+
+    def wide(c, which):
+        w, start, size = ((wqkv0, 0, part // 2), (wqkv0, part // 2, part // 2), (wqkv1, 0, part))[c]
+        return w.at[pl.ds(pl.multiple_of(which * part + start, 16), size), :]
+
+    def units(c, which, half):
+        at, quarter, start, size = (
+            (N_QKV, second, 0, second // 2),
+            (N_QKV, second, second // 2, second - second // 2),
+            (0, N_QKV // 4, 0, N_QKV // 8),
+            (0, N_QKV // 4, N_QKV // 8, N_QKV // 8),
+        )[c - 3]
+        return acc.at[pl.ds(half * N_HALF + at + which * quarter + start, size)]
+
+    def hop(kind, c):
+        which = q ^ 2 if kind == 3 else q
+        half = s if kind == 0 else 1 - s
+        ref = wide(c, which) if c < 3 else units(c, which, half)
+        return to(ref, ref, *flow(kind, c, which))
+
+    def only(c, sender):
+        if c in (3, 4):
+            return lambda do_it: do_it()
+        return pl.when(s == ((0 if sender else 1) if c < 3 else (1 if sender else 0)))
+
+    def launch(c):
+        @only(c, True)
+        def _():
+            hop(0, c).start()
+
+    def spread(c):
+        @only(c, False)
+        def _():
+            hop(0, c).wait_recv()
+            hop(1, c).start()
+            hop(2, c).start()
+
+    def pass_on(c):
+        @only(c, False)
+        def _():
+            hop(1, c).wait_recv()
+            hop(3, c).start()
+
+    def arrived(c):
+        @only(c, False)
+        def _():
+            hop(2, c).wait_recv()
+            hop(3, c).wait_recv()
+
+    def sent(c):
+        @only(c, True)
+        def _():
+            hop(0, c).wait_send()
+
+        @only(c, False)
+        def _():
+            for kind in (1, 2, 3):
+                hop(kind, c).wait_send()
+
     rest = acc.at[pl.ds(s * N_HALF + last, N_HALF - last)]
     rests = to(rest, rest, rest_sems.at[0], rest_sems.at[1], across)
+    launch(0)
+    launch(1)
     rests.start()
-    x_hops = [hop(0, c, s, q, across) for c in range(4)]
-    y_hops = [hop(1, c, 1 - s, q, beside) for c in range(4)]
-    core_hops = [hop(2, c, 1 - s, q, core) for c in range(4)]
-    far_hops = [hop(3, c, 1 - s, q ^ 2, core) for c in range(4)]
-    for copy in x_hops:
-        copy.start()
-
-    def spread(c):
-        x_hops[c].wait_recv()
-        y_hops[c].start()
-        core_hops[c].start()
-
-    def pass_on(c):
-        y_hops[c].wait_recv()
-        far_hops[c].start()
-
-    def arrived(c):
-        core_hops[c].wait_recv()
-        far_hops[c].wait_recv()
-
-    outs = [wqkv0, wo0, wup0, wdown0, vec0, wqkv1, wo1, wup1, wdown1, vec1]
-    flat = acc.reshape(2 * acc.shape[0], LANES)
+    top, low = pl.ds(0, x0.shape[0] // 2), pl.ds(x0.shape[0] // 2, x0.shape[0] // 2)
+    direct = to(a2.at[top], x0.at[top], swap_sems.at[0, 0], swap_sems.at[1, 0], diagonal)
+    aside = to(a2.at[low], do.at[low], relay_sems.at[0, 0], relay_sems.at[0, 1], core)
+    onward = to(do.at[low], x0.at[low], relay_sems.at[1, 0], relay_sems.at[1, 1], across)
+    local = pltpu.make_async_copy(a2, x0, load.at[1])
+
+    @pl.when(jnp.logical_not(stays))
+    def _():
+        aside.start()
+        direct.start()
+
+    @pl.when(stays)
+    def _():
+        local.start()
+        aside.wait_recv()
+        onward.start()
+
+    for c in (2, 3, 4, 5, 6):
+        launch(c)
+    spread(0)
+    spread(1)
     rests.wait_recv()
     unpack_small(flat, outs, main)
-    spread(0)
-    spread(1)
     pass_on(0)
     pass_on(1)
     arrived(0)
     arrived(1)
-    unpack_weights(flat, outs, main, 0)
-    spread(2)
 
     exchanges = []
 
@@ -620,19 +674,45 @@
         exchanges.append(copy)
         return copy
 
-    swapped(a2, x0, 0)
+
+    @pl.when(jnp.logical_not(stays))
+    def _():
+        aside.wait_send()
+        direct.wait()
+        onward.wait_recv()
+
+    @pl.when(stays)
+    def _():
+        local.wait()
+
     qkv_forward(x0, wqkv0, vec0, q0, kv0.at[0])
     first_kv = exchange(kv0.at[0], kv0.at[1])
+    spread(2)
     spread(3)
-    swap(dq, cot, 1)
+    pass_on(2)
     first_kv.wait_recv()
-    attend(q0, kv0, o_t0, lse0, values_t, rows)
-    pass_on(2)
-    pass_on(3)
-    arrived(2)
-    arrived(3)
-    for copy in x_hops + y_hops + core_hops + far_hops + [rests]:
-        copy.wait_send()
+
+    def relay(k):
+        spread(4 + k)
+        if k == 0:
+            swap(dq, cot, 1)
+        if k == 2:
+            pass_on(3)
+            pass_on(4)
+
+    attend(q0, kv0, o_t0, lse0, values_t, rows, relay)
+    pass_on(5)
+    pass_on(6)
+    for c in (2, 3, 4, 5, 6):
+        arrived(c)
+    for c in range(7):
+        sent(c)
+    rests.wait_send()
+
+    @pl.when(stays)
+    def _():
+        onward.wait_send()
+
     for which in (1, 2, 3):
         unpack_weights(flat, outs, main, which)
     out_forward(x0, o_t0, wo0, vec0, h10)
@@ -662,10 +742,13 @@
         to_low(main, half_rows - N_QKV, flat, base + N_QKV + moved, 32, 32)
         tail[...] = main[moved : moved + 32, :]
 
+    def late_start(layer):
+        to_low(main, 0, flat, layer * 2 * half_rows, N_QKV)
+        reducer.advance(late[layer][1:])
+
     def late_end(layer):
-        base = layer * 2 * half_rows
-        to_low(main, 0, flat, base, N_QKV)
-        to_low(tail, 0, flat, base + half_rows, 32, 32)
+        to_low(tail, 0, flat, layer * 2 * half_rows + half_rows, 32, 32)
+        reducer.advance(late[layer][:1])
 
     tail_shift = N_MAIN + shift - moved
     main_start()
@@ -675,13 +758,13 @@
     out_backward(shift, dh1, o_t1, wo1, main, do, delta)
     main_end(1)
     reducer.advance(early[1])
-    attend_backward(q1, kv1, lse1, do, delta, dq, dkv, dq_t, part_dk, part_dv, keys_t, rows,
+    attend_backward(q1, kv1, lse1, do, delta, dqkv, dkv_oth, dq_t, rows,
                     lambda hp: reducer.advance(early[1]))
-    exchange(dkv.at[1], dkv_in).wait_recv()
-    qkv_backward(tail_shift, x1, dq, dkv.at[0], dkv_in, dh1, wqkv1, vec1, main, tail, a2, da, h11)
+    exchange(dkv_oth, dkv_in).wait_recv()
+    qkv_backward(tail_shift, x1, dqkv, dkv_in, dh1, wqkv1, vec1, main, tail, a2, da, h11,
+                 lambda: late_start(1))
     late_end(1)
     reducer.advance(early[1])
-    reducer.advance(late[1])
     main_start()
     second_norm(h10, vec0, a2)
     reducer.advance(late[1])
@@ -692,17 +775,17 @@
     main_end(0)
     reducer.advance(late[1])
     reducer.advance(early[0])
-    attend_backward(q0, kv0, lse0, do, delta, dq, dkv, dq_t, part_dk, part_dv, keys_t, rows,
+    attend_backward(q0, kv0, lse0, do, delta, dqkv, dkv_oth, dq_t, rows,
                     lambda hp: reducer.advance(early[1] + late[1] + early[0]))
-    exchange(dkv.at[1], kv1.at[1]).wait_recv()
-    qkv_backward(tail_shift, x0, dq, dkv.at[0], kv1.at[1], dh1, wqkv0, vec0, main, tail, a2, da, do)
+    exchange(dkv_oth, kv1.at[1]).wait_recv()
+    qkv_backward(tail_shift, x0, dqkv, kv1.at[1], dh1, wqkv0, vec0, main, tail, a2, da, do,
+                 lambda: late_start(0))
     swap(do, cot, 3)
     late_end(0)
-    for tick in range(reducer.stages + 2):
-        reducer.advance(early[1] + late[1] + early[0])
-        for k, ci in enumerate(late[0]):
-            if tick >= k:
-                reducer.advance([ci])
+    others = early[0] + late[1] + early[1]
+    for tick in range(reducer.stages):
+        reducer.advance(late[0][::-1])
+        reducer.advance(others)
     reducer.drain()
     for k, copy in enumerate(exchanges):
         if k != 2:
@@ -746,8 +829,10 @@
         weight = flat(w_ref)[rows, :].astype(f32)
         one = beta_one * flat(one_ref)[rows, :] + (1.0 - beta_one) * grad
         two = beta_two * flat(two_ref)[rows, :] + (1.0 - beta_two) * grad * grad
-        step = (one * (1.0 / fix_one)) / (jnp.sqrt(two * (1.0 / fix_two)) + adam_eps) + decay * weight
-        flat(p_out)[rows, :] = weight - rate * step
+        square = two * (1.0 / fix_two)
+        root = square * lax.rsqrt(square)
+        step = one * lax.rsqrt(square + adam_eps * (2.0 * root + adam_eps))
+        flat(p_out)[rows, :] = weight * (1.0 - rate * decay) - (rate / fix_one) * step
         flat(one_out)[rows, :] = one
         flat(two_out)[rows, :] = two
 
@@ -783,7 +868,7 @@
     lse_f = vm((8, pad), f32)
     o_t_b = vm((D, pad), bf16)
     layer_w = [vm((D, 3 * D), bf16), vm((D, D), bf16), vm((D, FF), bf16), vm((FF, D), bf16), vm((VECS, D), f32)]
-    down, up = copies_of(ranks)
+    down, up = copies_of(levels_of(ranks, True))
     total = LAYERS * CHUNKS
     chunk_sems = pltpu.SemaphoreType.DMA((total, sum(down) + sum(up)))
     anywhere = pl.BlockSpec(memory_space=pl.ANY)
@@ -795,18 +880,18 @@
         out_specs=[inside] * 2 + [anywhere] * 2,
         scratch_shapes=[row_b, row_b] + layer_w * 2
         + [row_b, kv_both, o_t_b, lse_f, row_f, row_f, row_b, kv_both, o_t_b, lse_f, row_f, row_b]
-        + [row_f, row_f, row_b, lse_f, row_b, kv_both, kv_b]
-        + [vm((LANES, pad), f32), vm((pad, LANES), f32), vm((pad, LANES), f32), vm((LANES, pad), bf16), vm((LANES + 16, 2 * pad), bf16), row_b]
+        + [row_f, row_f, row_b, lse_f, row_b, vm((3, pad, D), bf16), kv_b, kv_b]
+        + [vm((LANES, pad), f32), vm((LANES + 16, 2 * pad), bf16), row_b]
         + [vm((N_MAIN + tail_rows, LANES), f32), vm((32, LANES), f32), vm((2 * half_rows, 2, LANES), bf16)]
         + [vm((half_rows, 2, LANES), bf16), vm((total, half_rows // CHUNKS, 2, LANES), bf16)]
         + [pltpu.SemaphoreType.DMA((5,)), pltpu.SemaphoreType.DMA((2,)), pltpu.SemaphoreType.DMA((2, 4))]
-        + [pltpu.SemaphoreType.DMA((2,)), pltpu.SemaphoreType.DMA((4, 2, 4)), pltpu.SemaphoreType.DMA((2, 4))]
+        + [pltpu.SemaphoreType.DMA((2, 2)), pltpu.SemaphoreType.DMA((2,)), pltpu.SemaphoreType.DMA((4, 2, 7)), pltpu.SemaphoreType.DMA((2, 4))]
         + [chunk_sems, chunk_sems],
         compiler_params=pltpu.CompilerParams(vmem_limit_bytes=67043328, collective_id=0, has_side_effects=True),
         name="step",
     )(frames_in[0], cotangent[0], w_rows)
     encoded, frames_grad = enc[None], dx[None]
-    block = 640
+    block = 1280
     low = pl.BlockSpec((block // 2, 2, LANES), lambda i: (i, 0, 0))
     spec = pl.BlockSpec((block, 2, LANES), lambda i: (i, 0, 0))
     row_shape = sd((N_HALF, 2, LANES), f32)

time: 258 us -> 233 us (0.903)
  Pallas kernels: 255 us -> 230 us
    pallas_call x1, Pallas kernels: 230 us -> 207 us  [body(): pl.pallas_call(partial(step_kernel, ranks, rows, half_rows), out_shape=[s...]
where the time goes in v1:
time: 233 us
  Pallas kernels  230 us (99%)
    pallas_call x1, Pallas kernels, body(): pl.pallas_call(partial(step_kernel, ranks, rows, half_rows), out_shape=[s...  207 us
    pallas_call x1, Pallas kernels, body(): pl.pallas_call(adam_kernel, grid=(pl.cdiv(N_HALF, block),), in_specs=[low...  23.2 us

profile of v1, /device:TPU:1, one launch (start us, length us, event | category | flops | bytes accessed | tf_op | source)
XLA Modules:
  0.0 232.6 jit_solution(7472508422735517042)
XLA Ops:
  0.6 207.2 %step.1 = (bf16[750,384]{1,0:T(8,128)(2,1)}, bf16[750,384]{1,0:T(8,128)(2,1)}, bf16[3584,2,128]{2,1,0:T(2,128)(2,1)}, bf16[3584,2,128]{2,1,0:T(2,128)(2,1)}) custom-call(bf16[750,384]{1,0:T(8,128)(2,1)} %bitcast.29, bf16[750,384]{1,0:T(8,128)(2,1)} %bitcast.30, bf16[6930,2,128]{2,1,0:T(2,128)(2,1)} %bitcast.25), custom_call_target="tpu_custom_call" | custom-call | tf_op jit(solution)/shard_map/step/pallas_call | solution.py:876
  207.8 0.0 copy-start.1
  207.8 0.0 copy-start
  207.8 23.2 %adam.1 = (f32[6930,2,128]{2,1,0:T(2,128)}, f32[6930,2,128]{2,1,0:T(2,128)}, f32[6930,2,128]{2,1,0:T(2,128)}, f32[6930,2,128]{2,1,0:T(2,128)}) custom-call(bf16[3584,2,128]{2,1,0:T(2,128)(2,1)} %get-tuple-element.16.g0_ref, bf16[3584,2,128]{2,1,0:T(2,128)(2,1)} %get-tuple-element.17.g1_ref, bf16[6930,2,128]{2,1,0:T(2,128)(2,1)} %bitcast.26, ...), custom_call_target="tpu_custom_call" | custom-call | tf_op jit(solution)/shard_map/adam/pallas_call | solution.py:898
  231.0 0.0 copy-done.1
  231.0 0.8 copy.13
  231.8 0.0 copy-done
  231.8 0.8 copy.14
Async XLA Ops:
  207.8 23.2 %copy-start.1 = (bf16[750,384]{1,0:T(8,128)(2,1)S(1)}, bf16[750,384]{1,0:T(8,128)(2,1)}, u32[]{:S(2)}) copy-start(bf16[750,384]{1,0:T(8,128)(2,1)} %get-tuple-element.14) | copy-start | bytes 1728004
  207.8 24.0 %copy-start = (bf16[750,384]{1,0:T(8,128)(2,1)S(1)}, bf16[750,384]{1,0:T(8,128)(2,1)}, u32[]{:S(2)}) copy-start(bf16[750,384]{1,0:T(8,128)(2,1)} %get-tuple-element.15) | copy-start | bytes 1728004

commit v2 on v1

--- a/solution.py
+++ b/solution.py
@@ -227,12 +227,13 @@
     return jnp.sum(values.astype(f32), axis=0, keepdims=True)
 
 
-def mlp_backward(shift, g_ref, h1_ref, a2_ref, wup_ref, wdown_ref, vec_ref, main_ref, da2_ref, dh1_ref, enc_ref):
+def mlp_backward(shift, g_ref, h1_ref, a2_ref, a_t_ref, wup_ref, wdown_ref, vec_ref, main_ref, da2_ref, dh1_ref, enc_ref):
     rows_all = g_ref.shape[0]
     small = N_MAIN + shift
     dy2 = g_ref[...].astype(bf16)
     put_row(main_ref, small + 21, column_sum(dy2))
     da2_ref[...] = jnp.zeros_like(da2_ref)
+    a_t_ref[...] = a2_ref[...].T
     if enc_ref is not None:
         dh1_ref[...] = h1_ref[...] + vec(vec_ref, BD)
 
@@ -248,7 +249,7 @@
         put_flat(main_ref, DOWN_BASE + shift + T_DOWN * FB * b, T_DOWN, tn(z, dy2))
         du = (nt(dy2, wdown_ref[cols, :]) * slope).astype(bf16)
         put_row(main_ref, small + 24 + 3 * b, column_sum(du))
-        put_up(main_ref, shift, b, tn(a2_ref[...], du))
+        put_up(main_ref, shift, b, nn(a_t_ref[...], du))
         da2_ref[...] += nt(du, wup_ref[:, cols])
 
     if enc_ref is not None:
@@ -311,7 +312,7 @@
 
 
 def qkv_backward(shift, x_ref, dqkv_ref, dkv_in_ref, dh1_ref, wqkv_ref, vec_ref, gq_ref, tail_ref,
-                 a_ref, da_ref, dx_ref, after_blocks):
+                 a_ref, a_t_ref, da_ref, dx_ref, after_blocks):
     def first(rows):
         xhat, _ = stats(x_ref[rows, :].astype(f32))
         a_ref[rows, :] = (xhat * vec(vec_ref, G1) + vec(vec_ref, N1)).astype(bf16)
@@ -320,6 +321,7 @@
             dqkv_ref[b + 1, rows, :] = total.astype(bf16)
 
     each_chunk(x_ref.shape[0], first)
+    a_t_ref[...] = a_ref[...].T
     da_ref[...] = jnp.zeros_like(da_ref)
 
     @pl.loop(0, 3)
@@ -330,7 +332,7 @@
         def _():
             put_row(tail_ref, shift + 9 + jnp.where(b == 2, 3, 0), column_sum(low))
 
-        put_flat(gq_ref, 3 * b, T_QKV, tn(a_ref[...], low))
+        put_flat(gq_ref, 3 * b, T_QKV, nn(a_t_ref[...], low))
         da_ref[...] += nt(low, wqkv_ref[:, pl.ds(pl.multiple_of(b * D, D), D)])
 
     after_blocks()
@@ -523,7 +525,7 @@
 
 def step_kernel(ranks, rows, half_rows, frames, cot_in, weights, enc_out, dx_out, out0, out1, x0, cot,
                 wqkv0, wo0, wup0, wdown0, vec0, wqkv1, wo1, wup1, wdown1, vec1,
-                q0, kv0, o_t0, lse0, h10, x1, q1, kv1, o_t1, lse1, h11, a2, da, dh1,
+                q0, kv0, o_t0, lse0, h10, x1, q1, kv1, o_t1, lse1, h11, a2, a_t, da, dh1,
                 do, delta, dq, dqkv, dkv_oth, dkv_in, dq_t, values_t, enc_in, main, tail, acc, res, landing,
                 load, store, swap_sems, relay_sems, rest_sems, hop_sems, kv_sems, send_sems, recv_sems):
     s, r = lax.axis_index("shard"), lax.axis_index("rep")
@@ -738,12 +740,13 @@
 
     def main_end(layer):
         base = layer * 2 * half_rows
-        to_low(main, 0, flat, base + N_QKV, main.shape[0])
+        to_low(main, 0, flat, base + N_QKV, N_MAIN, 192)
+        to_low(main, N_MAIN, flat, base + N_QKV + N_MAIN, main.shape[0] - N_MAIN)
         to_low(main, half_rows - N_QKV, flat, base + N_QKV + moved, 32, 32)
         tail[...] = main[moved : moved + 32, :]
 
     def late_start(layer):
-        to_low(main, 0, flat, layer * 2 * half_rows, N_QKV)
+        to_low(main, 0, flat, layer * 2 * half_rows, N_QKV, 192)
         reducer.advance(late[layer][1:])
 
     def late_end(layer):
@@ -753,7 +756,7 @@
     tail_shift = N_MAIN + shift - moved
     main_start()
     swapped(dq, cot, 1)
-    mlp_backward(shift, cot, h11, a2, wup1, wdown1, vec1, main, da, dh1, enc)
+    mlp_backward(shift, cot, h11, a2, a_t, wup1, wdown1, vec1, main, da, dh1, enc)
     swap(enc, enc_in, 2)
     out_backward(shift, dh1, o_t1, wo1, main, do, delta)
     main_end(1)
@@ -761,7 +764,7 @@
     attend_backward(q1, kv1, lse1, do, delta, dqkv, dkv_oth, dq_t, rows,
                     lambda hp: reducer.advance(early[1]))
     exchange(dkv_oth, dkv_in).wait_recv()
-    qkv_backward(tail_shift, x1, dqkv, dkv_in, dh1, wqkv1, vec1, main, tail, a2, da, h11,
+    qkv_backward(tail_shift, x1, dqkv, dkv_in, dh1, wqkv1, vec1, main, tail, a2, a_t, da, h11,
                  lambda: late_start(1))
     late_end(1)
     reducer.advance(early[1])
@@ -769,7 +772,7 @@
     second_norm(h10, vec0, a2)
     reducer.advance(late[1])
     exchanges[-1].wait_send()
-    mlp_backward(shift, h11, h10, a2, wup0, wdown0, vec0, main, da, dh1, None)
+    mlp_backward(shift, h11, h10, a2, a_t, wup0, wdown0, vec0, main, da, dh1, None)
     reducer.advance(early[1])
     out_backward(shift, dh1, o_t0, wo0, main, do, delta)
     main_end(0)
@@ -778,7 +781,7 @@
     attend_backward(q0, kv0, lse0, do, delta, dqkv, dkv_oth, dq_t, rows,
                     lambda hp: reducer.advance(early[1] + late[1] + early[0]))
     exchange(dkv_oth, kv1.at[1]).wait_recv()
-    qkv_backward(tail_shift, x0, dqkv, kv1.at[1], dh1, wqkv0, vec0, main, tail, a2, da, do,
+    qkv_backward(tail_shift, x0, dqkv, kv1.at[1], dh1, wqkv0, vec0, main, tail, a2, a_t, da, do,
                  lambda: late_start(0))
     swap(do, cot, 3)
     late_end(0)
@@ -879,7 +882,7 @@
         in_specs=[inside, inside, anywhere],
         out_specs=[inside] * 2 + [anywhere] * 2,
         scratch_shapes=[row_b, row_b] + layer_w * 2
-        + [row_b, kv_both, o_t_b, lse_f, row_f, row_f, row_b, kv_both, o_t_b, lse_f, row_f, row_b]
+        + [row_b, kv_both, o_t_b, lse_f, row_f, row_f, row_b, kv_both, o_t_b, lse_f, row_f, row_b, o_t_b]
         + [row_f, row_f, row_b, lse_f, row_b, vm((3, pad, D), bf16), kv_b, kv_b]
         + [vm((LANES, pad), f32), vm((LANES + 16, 2 * pad), bf16), row_b]
         + [vm((N_MAIN + tail_rows, LANES), f32), vm((32, LANES), f32), vm((2 * half_rows, 2, LANES), bf16)]

time: 233 us -> 244 us (1.047); the launches traced: 233 us -> 240 us
  Pallas kernels: 230 us -> 237 us
    pallas_call x1, Pallas kernels: 207 us -> 214 us  [body(): pl.pallas_call(partial(step_kernel, ranks, rows, half_rows), out_shape=[s...]
where the time goes in v2:
time: 244 us; the launch traced here: 240 us
  Pallas kernels  237 us (97%)
    pallas_call x1, Pallas kernels, body(): pl.pallas_call(partial(step_kernel, ranks, rows, half_rows), out_shape=[s...  214 us
    pallas_call x1, Pallas kernels, body(): pl.pallas_call(adam_kernel, grid=(pl.cdiv(N_HALF, block),), in_specs=[low...  23.2 us

profile of v2, /device:TPU:1, one launch (start us, length us, event | category | flops | bytes accessed | tf_op | source)
XLA Modules:
  0.0 239.8 jit_solution(12038643833834308488)
XLA Ops:
  0.6 214.1 %step.1 = (bf16[750,384]{1,0:T(8,128)(2,1)}, bf16[750,384]{1,0:T(8,128)(2,1)}, bf16[3584,2,128]{2,1,0:T(2,128)(2,1)}, bf16[3584,2,128]{2,1,0:T(2,128)(2,1)}) custom-call(bf16[750,384]{1,0:T(8,128)(2,1)} %bitcast.29, bf16[750,384]{1,0:T(8,128)(2,1)} %bitcast.30, bf16[6930,2,128]{2,1,0:T(2,128)(2,1)} %bitcast.25), custom_call_target="tpu_custom_call" | custom-call | tf_op jit(solution)/shard_map/step/pallas_call | solution.py:879
  214.8 0.0 copy-start.1
  214.8 0.0 copy-start
  214.8 23.2 %adam.1 = (f32[6930,2,128]{2,1,0:T(2,128)}, f32[6930,2,128]{2,1,0:T(2,128)}, f32[6930,2,128]{2,1,0:T(2,128)}, f32[6930,2,128]{2,1,0:T(2,128)}) custom-call(bf16[3584,2,128]{2,1,0:T(2,128)(2,1)} %get-tuple-element.16.g0_ref, bf16[3584,2,128]{2,1,0:T(2,128)(2,1)} %get-tuple-element.17.g1_ref, bf16[6930,2,128]{2,1,0:T(2,128)(2,1)} %bitcast.26, ...), custom_call_target="tpu_custom_call" | custom-call | tf_op jit(solution)/shard_map/adam/pallas_call | solution.py:901
  238.0 0.0 copy-done.1
  238.0 0.8 copy.13
  238.8 0.0 copy-done
  238.8 0.8 copy.14
Async XLA Ops:
  214.8 23.2 %copy-start.1 = (bf16[750,384]{1,0:T(8,128)(2,1)S(1)}, bf16[750,384]{1,0:T(8,128)(2,1)}, u32[]{:S(2)}) copy-start(bf16[750,384]{1,0:T(8,128)(2,1)} %get-tuple-element.14) | copy-start | bytes 1728004
  214.8 24.0 %copy-start = (bf16[750,384]{1,0:T(8,128)(2,1)S(1)}, bf16[750,384]{1,0:T(8,128)(2,1)}, u32[]{:S(2)}) copy-start(bf16[750,384]{1,0:T(8,128)(2,1)} %get-tuple-element.15) | copy-start | bytes 1728004

commit v3 on v2

--- a/solution.py
+++ b/solution.py
@@ -113,13 +113,13 @@
             pl.ds(pl.multiple_of(2 * base + i * 384, 128), 384), :
         ].astype(f32)
 
-    @pl.loop(0, count // tiles // 128)
+    @pl.loop(0, count // tiles // 64)
     def _(i):
         for layer in range(LAYERS):
             for j in range(tiles):
                 outs[5 * layer + which][
-                    pl.ds(pl.multiple_of(i * 128, 128), 128), j * LANES : (j + 1) * LANES
-                ] = stage[pl.ds(i * (256 * tiles) + 2 * j + layer, 128, stride=2 * tiles), :].astype(bf16)
+                    pl.ds(pl.multiple_of(i * 64, 64), 64), j * LANES : (j + 1) * LANES
+                ] = stage[pl.ds(i * (128 * tiles) + 2 * j + layer, 64, stride=2 * tiles), :].astype(bf16)
 
 
 def unpack_small(flat, outs, stage):
@@ -740,13 +740,13 @@
 
     def main_end(layer):
         base = layer * 2 * half_rows
-        to_low(main, 0, flat, base + N_QKV, N_MAIN, 192)
+        to_low(main, 0, flat, base + N_QKV, N_MAIN)
         to_low(main, N_MAIN, flat, base + N_QKV + N_MAIN, main.shape[0] - N_MAIN)
         to_low(main, half_rows - N_QKV, flat, base + N_QKV + moved, 32, 32)
         tail[...] = main[moved : moved + 32, :]
 
     def late_start(layer):
-        to_low(main, 0, flat, layer * 2 * half_rows, N_QKV, 192)
+        to_low(main, 0, flat, layer * 2 * half_rows, N_QKV)
         reducer.advance(late[layer][1:])
 
     def late_end(layer):

time: 244 us -> 233 us (0.955); the launches traced: 240 us -> 233 us
  Pallas kernels: 237 us -> 231 us
    pallas_call x1, Pallas kernels: 214 us -> 207 us  [body(): pl.pallas_call(partial(step_kernel, ranks, rows, half_rows), out_shape=[s...]
where the time goes in v3:
time: 233 us
  Pallas kernels  231 us (99%)
    pallas_call x1, Pallas kernels, body(): pl.pallas_call(partial(step_kernel, ranks, rows, half_rows), out_shape=[s...  207 us
    pallas_call x1, Pallas kernels, body(): pl.pallas_call(adam_kernel, grid=(pl.cdiv(N_HALF, block),), in_specs=[low...  23.2 us

profile of v3, /device:TPU:1, one launch (start us, length us, event | category | flops | bytes accessed | tf_op | source)
XLA Modules:
  0.0 232.9 jit_solution(15620349734994522790)
XLA Ops:
  0.6 207.4 %step.1 = (bf16[750,384]{1,0:T(8,128)(2,1)}, bf16[750,384]{1,0:T(8,128)(2,1)}, bf16[3584,2,128]{2,1,0:T(2,128)(2,1)}, bf16[3584,2,128]{2,1,0:T(2,128)(2,1)}) custom-call(bf16[750,384]{1,0:T(8,128)(2,1)} %bitcast.29, bf16[750,384]{1,0:T(8,128)(2,1)} %bitcast.30, bf16[6930,2,128]{2,1,0:T(2,128)(2,1)} %bitcast.25), custom_call_target="tpu_custom_call" | custom-call | tf_op jit(solution)/shard_map/step/pallas_call | solution.py:879
  208.1 0.0 copy-start.1
  208.1 0.0 copy-start
  208.1 23.2 %adam.1 = (f32[6930,2,128]{2,1,0:T(2,128)}, f32[6930,2,128]{2,1,0:T(2,128)}, f32[6930,2,128]{2,1,0:T(2,128)}, f32[6930,2,128]{2,1,0:T(2,128)}) custom-call(bf16[3584,2,128]{2,1,0:T(2,128)(2,1)} %get-tuple-element.16.g0_ref, bf16[3584,2,128]{2,1,0:T(2,128)(2,1)} %get-tuple-element.17.g1_ref, bf16[6930,2,128]{2,1,0:T(2,128)(2,1)} %bitcast.26, ...), custom_call_target="tpu_custom_call" | custom-call | tf_op jit(solution)/shard_map/adam/pallas_call | solution.py:901
  231.3 0.0 copy-done.1
  231.3 0.8 copy.13
  232.1 0.0 copy-done
  232.1 0.8 copy.14
Async XLA Ops:
  208.1 23.2 %copy-start.1 = (bf16[750,384]{1,0:T(8,128)(2,1)S(1)}, bf16[750,384]{1,0:T(8,128)(2,1)}, u32[]{:S(2)}) copy-start(bf16[750,384]{1,0:T(8,128)(2,1)} %get-tuple-element.14) | copy-start | bytes 1728004
  208.1 24.0 %copy-start = (bf16[750,384]{1,0:T(8,128)(2,1)S(1)}, bf16[750,384]{1,0:T(8,128)(2,1)}, u32[]{:S(2)}) copy-start(bf16[750,384]{1,0:T(8,128)(2,1)} %get-tuple-element.15) | copy-start | bytes 1728004
